TPU v7x, 256 devices: a whole 4x4x8 slice. The times are simulated.
256 devices in a mesh: vrow: 32 (over z, y), vcol: 8 (over x, core).
Axes of the slice: x: 4, y: 4, z: 8, core: 2. Of those that a mesh axis runs over, the one named last changes fastest.
Arguments:
- policy_hidden: bfloat16 [1024, 3584], P(None, 'vcol'), may hold values from -400 to 400
- ref_hidden: bfloat16 [1024, 3584], P(None, 'vcol'), may hold values from -400 to 400
- mix_num: int32 [1024], replicated, may hold values from 0 to 16, as said below
- mix_den: int32 [1024], replicated, may hold values from 2 to 16
- policy_unembed: bfloat16 [3584, 131072], P(None, ('vrow', 'vcol')), may hold values from -0.09375 to 0.09375
- ref_unembed: bfloat16 [3584, 131072], P(None, ('vrow', 'vcol')), may hold values from -0.09375 to 0.09375
Outputs:
- mix_logprobs: float32 [1024, 131072], P(None, ('vrow', 'vcol'))
Inputs may be any that keep to these rules, and one draw needn't show every extreme that they name: Each sequence's mix_num is at most its mix_den.
All inputs are finite; a program needn't handle non-finite values.
Results may differ from a plain program's by a relative error of at most 0.0003.
Values may be sent and summed in bfloat16 or wider, within the bound.
A program may use at most 64 MiB of HBM per device.

v0:
```python
import jax
import jax.numpy as jnp
from jax import lax
from jax.sharding import Mesh
from jax.sharding import PartitionSpec as P

VCOL = ("vcol_0", "vcol_1")
VROW_VCOL = ("vrow_0", "vrow_1", "vcol_0", "vcol_1")


def rows_first(arrays, axis, dims):
    turned = [jnp.moveaxis(a, dim, 0) for a, dim in zip(arrays, dims)]
    both = jnp.concatenate([t.reshape(len(t), -1) for t in turned], axis=1)
    filled, at, done = (lax.all_gather(both, axis, axis=0, tiled=True), 0, [])
    for t, dim in zip(turned, dims):
        slab = filled[:, at : at + t[0].size].reshape(-1, *t.shape[1:])
        done.append(jnp.moveaxis(slab, 0, dim))
        at += t[0].size
    return tuple(done)


def collected_together(value, axis):
    leaves = jax.tree.leaves(value)
    order = sorted(range(len(leaves)), key=lambda k: -leaves[k].size)
    width = (1, *leaves[order[0]].shape)[-1]
    lines = [
        jnp.pad(leaves[k].reshape(-1), (0, -leaves[k].size % width)).reshape(-1, width)
        for k in order
    ]
    both, at, found = (lax.all_gather(jnp.concatenate(lines), axis), 0, {})
    for k, line in zip(order, lines):
        slab = both[:, at : at + len(line)].reshape(len(both), -1)
        found[k] = slab[:, : leaves[k].size].reshape(-1, *leaves[k].shape)
        at += len(line)
    numbers = iter(range(len(leaves)))
    return jax.tree.map(lambda _: found[next(numbers)], value)


def joined_all(value, axes, combine):
    for axis in axes:
        pieces = collected_together(value, axis)
        value = jax.tree.map(lambda part: part[0], pieces)
        for k in range(1, lax.axis_size(axis)):
            value = combine(value, jax.tree.map(lambda part: part[k], pieces))
    return value


def combine_stats(first, second):
    high = jnp.maximum(first[0], second[0])
    total = first[1] * jnp.exp(first[0] - high) + second[1] * jnp.exp(second[0] - high)
    return (high, total)


def body(policy_hidden, ref_hidden, mix_num, mix_den, policy_unembed, ref_unembed):
    policy_full, ref_full = rows_first((policy_hidden, ref_hidden), VCOL, (1, 1))
    policy_logits = jnp.dot(policy_full, policy_unembed, preferred_element_type=jnp.float32)
    ref_logits = jnp.dot(ref_full, ref_unembed, preferred_element_type=jnp.float32)
    beta = (mix_num.astype(jnp.float32) / mix_den.astype(jnp.float32))[:, None]
    mixed = (1.0 - beta) * policy_logits + beta * ref_logits
    local_top = jnp.max(mixed, axis=1, keepdims=True)
    local_total = jnp.sum(jnp.exp(mixed - local_top), axis=1, keepdims=True)
    top, total = joined_all((local_top, local_total), VROW_VCOL, combine_stats)
    return mixed - top - jnp.log(total)


def solution(mesh):
    finer = Mesh(mesh.devices.reshape(8, 4, 4, 2), ("vrow_0", "vrow_1", "vcol_0", "vcol_1"))
    placed = (P(None, VCOL), P(None, VCOL), P(), P(), P(None, VROW_VCOL), P(None, VROW_VCOL))
    return jax.shard_map(
        body, mesh=finer, in_specs=placed, out_specs=P(None, VROW_VCOL), check_vma=False
    )
```

profile of v0, /device:TPU:1, one launch (start us, length us, event | category | flops | bytes accessed | tf_op | source)
XLA Modules:
  0.0 172.9 jit_solution(6092440054672598661)
XLA Ops:
  6.5 0.0 all-gather.6.cloned.1.call-start
  6.5 0.0 copy-start
  6.5 0.0 copy-start.1
  6.5 2.9 %pad_maximum_fusion = bf16[448,2048]{1,0:T(8,128)(2,1)} fusion(bf16[448,1024]{1,0:T(8,128)(2,1)} %bitcast.319, bf16[448,1024]{1,0:T(8,128)(2,1)} %bitcast.320), kind=kLoop, calls=%fused_computation.7 | loop fusion | flops 3670016 | bytes 3670016 | tf_op jit(solution)/shard_map/concatenate | solution.py:13
  9.4 0.0 all-gather.6.cloned.1.call-update
  9.5 0.0 copy-done
  9.5 0.0 copy-done.1
  9.5 82.9 %all-gather.6.cloned.1.call-done = bf16[3584,2048]{1,0:T(8,128)(2,1)} async-done(((bf16[448,2048]{1,0:T(8,128)(2,1)}), bf16[3584,2048]{1,0:T(8,128)(2,1)}) %all-gather.6.cloned.1.call-update) | async-done | bytes 14680080 | tf_op jit(solution)/shard_map/all_gather | solution.py:14
  92.4 0.0 copy-start.2
  92.4 0.0 copy-start.3
  92.4 7.5 %fusion = f32[1024,512]{0,1:T(8,128)S(1)} fusion(bf16[3584,512]{1,0:T(8,128)(2,1)} %param.11, bf16[3584,2048]{1,0:T(8,128)(2,1)} %all-gather.6.cloned.1.call-done), kind=kOutput, calls=%fused_computation | convolution fusion | flops 3758096384 | bytes 13107200 | tf_op jit(solution)/shard_map/dot_general | solution.py:57
  100.0 0.8 copy-done.2
  100.8 1.0 copy-done.3
  101.9 4.1 %fusion.62 = (f32[1024]{0:T(1024)S(1)}, f32[1024,512]{0,1:T(8,128)S(1)}) fusion(f32[1024,512]{0,1:T(8,128)S(1)} %fusion, f32[1024]{0:T(1024)S(1)} %get-tuple-element.14, bf16[3584,512]{1,0:T(8,128)(2,1)S(1)} %copy-done.3, bf16[3584,2048]{1,0:T(8,128)(2,1)S(1)} %copy-done.2, f32[1024]{0:T(1024)S(1)} %get-tuple-element.13), kind=kOutput, calls=%fused_computation.100 | convolution fusion | flops 3760192512 | bytes 15216640 | tf_op jit(solution)/shard_map/dot_general | solution.py:56
  106.0 0.3 exponential_reduce_fusion
  106.3 19.7 %all-gather = f32[16384,1]{0,1:T(1,128)S(1)} all-gather(f32[2048,1]{0,1:T(1,128)S(1)} %pad_maximum_fusion.1), channel_id=2, replica_groups=mesh['vrow_0'=8,'vrow_1'=4,'vcol_0'=4,'vcol_1'=2] {'vrow_0'}, dimensions={0}, use_global_device_ids=true | all-gather | bytes 73728 | tf_op jit(solution)/shard_map/all_gather | solution.py:30
  126.1 0.1 fusion.25
  126.2 9.5 %all-gather.1 = f32[8192,1]{0,1:T(1,128)S(1)} all-gather(f32[2048,1]{0,1:T(1,128)S(1)} %pad_maximum_fusion.2), channel_id=3, replica_groups=mesh['vrow_0'=8,'vrow_1'=4,'vcol_0'=4,'vcol_1'=2] {'vrow_1'}, dimensions={0}, use_global_device_ids=true | all-gather | bytes 40960 | tf_op jit(solution)/shard_map/all_gather | solution.py:30
  135.7 0.5 broadcast.16
  136.2 0.7 reduce.12
  137.0 0.1 fusion.16
  137.1 9.0 %all-gather.2 = f32[8192,1]{0,1:T(1,128)S(1)} all-gather(f32[2048,1]{0,1:T(1,128)S(1)} %pad_maximum_fusion.3), channel_id=4, replica_groups=mesh['vrow_0'=8,'vrow_1'=4,'vcol_0'=4,'vcol_1'=2] {'vcol_0'}, dimensions={0}, use_global_device_ids=true | all-gather | bytes 40960 | tf_op jit(solution)/shard_map/all_gather | solution.py:30
  146.1 0.7 reduce.13
  146.9 0.1 fusion.7
  146.9 13.7 %all-gather.3 = f32[4096,1]{0,1:T(1,128)S(1)} all-gather(f32[2048,1]{0,1:T(1,128)S(1)} %pad_maximum_fusion.4), channel_id=5, replica_groups=mesh['vrow_0'=8,'vrow_1'=4,'vcol_0'=4,'vcol_1'=2] {'vcol_1'}, dimensions={0}, use_global_device_ids=true | all-gather | bytes 24576 | tf_op jit(solution)/shard_map/all_gather | solution.py:30
  160.6 0.7 reduce.14
  161.4 1.8 %subtract_subtract_fusion = f32[1024,512]{0,1:T(8,128)} fusion(f32[1024,512]{0,1:T(8,128)S(1)} %get-tuple-element.20, f32[1024]{0:T(1024)S(1)} %get-tuple-element.5, f32[1024]{0:T(1024)S(1)} %get-tuple-element.6), kind=kLoop, calls=%fused_computation.4 | loop fusion | flops 1048576 | bytes 4202496 | tf_op jit(solution)/shard_map/sub | solution.py:63
  163.1 2.9 %copy.8 = f32[1024,512]{1,0:T(8,128)} copy(f32[1024,512]{0,1:T(8,128)} %subtract_subtract_fusion) | data formatting | bytes 4194304 | tf_op jit(solution)/shard_map/sub | solution.py:63
  (11 shorter events, 0.1 us)
Async XLA Ops:
  6.5 85.9 %all-gather.6.cloned.1.call-start = ((), (), s32[]{:S(2)}) async-start(), calls=%async_computation | async-start | bytes 16515072 | tf_op jit(solution)/shard_map/all_gather | solution.py:14
  6.5 2.9 %copy-start = (s32[1024]{0:T(1024)S(1)}, s32[1024]{0:T(1024)}, u32[]{:S(2)}) copy-start(s32[1024]{0:T(1024)} %param.9) | copy-start | bytes 12292
  6.5 2.9 %copy-start.1 = (s32[1024]{0:T(1024)S(1)}, s32[1024]{0:T(1024)}, u32[]{:S(2)}) copy-start(s32[1024]{0:T(1024)} %param.8) | copy-start | bytes 12292
  92.4 8.4 %copy-start.2 = (bf16[3584,2048]{1,0:T(8,128)(2,1)S(1)}, bf16[3584,2048]{1,0:T(8,128)(2,1)}, u32[]{:S(2)}) copy-start(bf16[3584,2048]{1,0:T(8,128)(2,1)} %all-gather.6.cloned.1.call-done) | copy-start | bytes 44040196
  92.4 9.4 %copy-start.3 = (bf16[3584,512]{1,0:T(8,128)(2,1)S(1)}, bf16[3584,512]{1,0:T(8,128)(2,1)}, u32[]{:S(2)}) copy-start(bf16[3584,512]{1,0:T(8,128)(2,1)} %param.10) | copy-start | bytes 11010052
Sparse Core Ops, SparseCore 0:
  9.6 82.7 all-gather.5
where the time goes:
time: 173 us
  waiting for transfers between devices  82.9 us (48%)
  blocking collectives  52 us (30%)
  between operations  13.5 us (8%)
  matrix products  11.7 us (7%)
  other arithmetic  7.39 us (4%)
  local copies, waits for them, and re-layouts  5.37 us (3%)
    all_gather x1, waiting for transfers between devices, rows_first(): filled, at, done = (lax.all_gather(both, axis, axis=0, tiled=True), 0, [])  82.9 us
    all_gather x4, blocking collectives, collected_together(): both, at, found = (lax.all_gather(jnp.concatenate(lines), axis), 0, {})  52 us
    dot_general x1, matrix products, body(): jnp.dot(ref_full, ref_unembed, preferred_element_type=jnp.float32)  7.54 us
    dot_general x1, matrix products, body(): jnp.dot(policy_full, policy_unembed, preferred_element_type=jnp.float32)  4.12 us
  transfers between devices with their start and end apart: 1, of which 1 were waited for; matrix products, arithmetic and copies ran while one was open for 0% of the time, Pallas kernels for 0%

commit v1 on v0

--- a/solution.py
+++ b/solution.py
@@ -3,6 +3,7 @@
 from jax import lax
 from jax.sharding import Mesh
 from jax.sharding import PartitionSpec as P
+from jax.lax import all_to_all, psum
 
 VCOL = ("vcol_0", "vcol_1")
 VROW_VCOL = ("vrow_0", "vrow_1", "vcol_0", "vcol_1")
@@ -11,7 +12,11 @@
 def rows_first(arrays, axis, dims):
     turned = [jnp.moveaxis(a, dim, 0) for a, dim in zip(arrays, dims)]
     both = jnp.concatenate([t.reshape(len(t), -1) for t in turned], axis=1)
-    filled, at, done = (lax.all_gather(both, axis, axis=0, tiled=True), 0, [])
+    filled, at, done = (
+        jnp.concatenate(all_to_all(jnp.stack([both for _ in range(psum(1, axis))]), axis, 0, 0), 0),
+        0,
+        [],
+    )
     for t, dim in zip(turned, dims):
         slab = filled[:, at : at + t[0].size].reshape(-1, *t.shape[1:])
         done.append(jnp.moveaxis(slab, 0, dim))

time: 173 us -> 253 us (1.46)
  waiting for transfers between devices: 82.9 us -> 161 us
  between operations: 13.5 us -> 0.15 us
  starting transfers between devices: 0.01 us -> 8.76 us
  local copies, waits for them, and re-layouts: 5.37 us -> 9.05 us
    all_to_all x0 -> x1, waiting for transfers between devices: none -> 161 us  [rows_first(): all_to_all(jnp.stack([both for _ in range(psum(1, axis))]), axis, 0, 0)]
    all_gather x1 -> x0, waiting for transfers between devices: 82.9 us -> none  [rows_first(): filled, at, done = (lax.all_gather(both, axis, axis=0, tiled=True), 0, [])]
    all_to_all x0 -> x1, starting transfers between devices: none -> 8.76 us  [rows_first(): all_to_all(jnp.stack([both for _ in range(psum(1, axis))]), axis, 0, 0)]
    another operation x0 -> x1, local copies, waits for them, and re-layouts: none -> 5.56 us  [rows_first(): jnp.stack([both for _ in range(psum(1, axis))])]
where the time goes in v1:
time: 253 us; the launch traced here: 252 us
  waiting for transfers between devices  161 us (64%)
  blocking collectives  53.3 us (21%)
  matrix products  13.9 us (5%)
  local copies, waits for them, and re-layouts  9.05 us (4%)
  starting transfers between devices  8.76 us (3%)
  other arithmetic  6.13 us (2%)
    all_to_all x1, waiting for transfers between devices, rows_first(): all_to_all(jnp.stack([both for _ in range(psum(1, axis))]), axis, 0, 0)  161 us
    all_gather x4, blocking collectives, collected_together(): both, at, found = (lax.all_gather(jnp.concatenate(lines), axis), 0, {})  53.3 us
    all_to_all x1, starting transfers between devices, rows_first(): all_to_all(jnp.stack([both for _ in range(psum(1, axis))]), axis, 0, 0)  8.76 us
    dot_general x1, matrix products, body(): jnp.dot(ref_full, ref_unembed, preferred_element_type=jnp.float32)  7.55 us
    dot_general x1, matrix products, body(): jnp.dot(policy_full, policy_unembed, preferred_element_type=jnp.float32)  6.35 us
    another operation x1, local copies, waits for them, and re-layouts, rows_first(): jnp.stack([both for _ in range(psum(1, axis))])  5.56 us
  transfers between devices with their start and end apart: 1, of which 1 were waited for; matrix products, arithmetic and copies ran while one was open for 0% of the time, Pallas kernels for 0%

profile of v1, /device:TPU:1, one launch (start us, length us, event | category | flops | bytes accessed | tf_op | source)
XLA Modules:
  0.0 252.4 jit_solution(15345800456918349386)
XLA Ops:
  0.0 1.6 pad_maximum_fusion
  1.6 5.6 %stack.2 = bf16[8,448,2048]{2,1,0:T(8,128)(2,1)} broadcast(bf16[448,2048]{1,0:T(8,128)(2,1)S(1)} %pad_maximum_fusion), dimensions={1,2} | broadcast | bytes 16515072 | tf_op jit(solution)/shard_map/stack | solution.py:16
  7.2 0.0 copy-start
  7.2 0.0 copy-start.1
  7.2 8.8 %all-to-all-start = ((bf16[8,448,2048]{2,1,0:T(8,128)(2,1)}), bf16[8,448,2048]{2,1,0:T(8,128)(2,1)}, u32[]{:S(2)}, u32[]{:S(2)}) async-start(bf16[8,448,2048]{2,1,0:T(8,128)(2,1)} %stack.2), calls=%async_computation | async-start | bytes 29360128 | tf_op jit(solution)/shard_map/all_to_all | solution.py:16
  16.0 0.0 copy-done
  16.0 0.0 copy-done.1
  16.0 161.1 %all-to-all-done = bf16[8,448,2048]{2,1,0:T(8,128)(2,1)} async-done(((bf16[8,448,2048]{2,1,0:T(8,128)(2,1)}), bf16[8,448,2048]{2,1,0:T(8,128)(2,1)}, u32[]{:S(2)}, u32[]{:S(2)}) %all-to-all-start) | async-done | bytes 14680096 | tf_op jit(solution)/shard_map/all_to_all | solution.py:16
  177.1 0.0 copy-start.2
  177.1 7.5 %fusion = f32[1024,512]{0,1:T(8,128)S(1)} fusion(bf16[3584,512]{1,0:T(8,128)(2,1)} %param.11, bf16[3584,2048]{1,0:T(8,128)(2,1)} %bitcast.2), kind=kOutput, calls=%fused_computation | convolution fusion | flops 3758096384 | bytes 13107200 | tf_op jit(solution)/shard_map/dot_general | solution.py:62
  184.7 0.0 copy-done.2
  184.7 6.4 %fusion.62 = (f32[1024]{0:T(1024)S(1)}, f32[1024,512]{0,1:T(8,128)S(1)}) fusion(f32[1024,512]{0,1:T(8,128)S(1)} %fusion, f32[1024]{0:T(1024)S(1)} %get-tuple-element.14, bf16[3584,512]{1,0:T(8,128)(2,1)S(1)} %copy-done.2, bf16[3584,2048]{1,0:T(8,128)(2,1)} %bitcast.2, f32[1024]{0:T(1024)S(1)} %get-tuple-element.13), kind=kOutput, calls=%fused_computation.100 | convolution fusion | flops 3760192512 | bytes 15216640 | tf_op jit(solution)/shard_map/dot_general | solution.py:61
  191.1 0.3 exponential_reduce_fusion
  191.4 20.2 %all-gather = f32[16384,1]{0,1:T(1,128)S(1)} all-gather(f32[2048,1]{0,1:T(1,128)S(1)} %pad_maximum_fusion.1), channel_id=2, replica_groups=mesh['vrow_0'=8,'vrow_1'=4,'vcol_0'=4,'vcol_1'=2] {'vrow_0'}, dimensions={0}, use_global_device_ids=true | all-gather | bytes 73728 | tf_op jit(solution)/shard_map/all_gather | solution.py:35
  211.7 0.1 fusion.25
  211.8 9.5 %all-gather.1 = f32[8192,1]{0,1:T(1,128)S(1)} all-gather(f32[2048,1]{0,1:T(1,128)S(1)} %pad_maximum_fusion.2), channel_id=3, replica_groups=mesh['vrow_0'=8,'vrow_1'=4,'vcol_0'=4,'vcol_1'=2] {'vrow_1'}, dimensions={0}, use_global_device_ids=true | all-gather | bytes 40960 | tf_op jit(solution)/shard_map/all_gather | solution.py:35
  221.3 0.5 broadcast.18
  221.8 0.7 reduce.12
  222.6 0.1 fusion.16
  222.7 9.0 %all-gather.2 = f32[8192,1]{0,1:T(1,128)S(1)} all-gather(f32[2048,1]{0,1:T(1,128)S(1)} %pad_maximum_fusion.3), channel_id=4, replica_groups=mesh['vrow_0'=8,'vrow_1'=4,'vcol_0'=4,'vcol_1'=2] {'vcol_0'}, dimensions={0}, use_global_device_ids=true | all-gather | bytes 40960 | tf_op jit(solution)/shard_map/all_gather | solution.py:35
  231.7 0.7 reduce.13
  232.5 0.1 fusion.7
  232.5 14.5 %all-gather.3 = f32[4096,1]{0,1:T(1,128)S(1)} all-gather(f32[2048,1]{0,1:T(1,128)S(1)} %pad_maximum_fusion.4), channel_id=5, replica_groups=mesh['vrow_0'=8,'vrow_1'=4,'vcol_0'=4,'vcol_1'=2] {'vcol_1'}, dimensions={0}, use_global_device_ids=true | all-gather | bytes 24576 | tf_op jit(solution)/shard_map/all_gather | solution.py:35
  247.0 0.7 reduce.14
  247.8 1.8 subtract_subtract_fusion
  249.6 2.9 %copy.8 = f32[1024,512]{1,0:T(8,128)} copy(f32[1024,512]{0,1:T(8,128)} %subtract_subtract_fusion) | data formatting | bytes 4194304 | tf_op jit(solution)/shard_map/sub | solution.py:68
  (11 shorter events, 0.1 us)
Async XLA Ops:
  7.2 8.8 %copy-start = (s32[1024]{0:T(1024)S(1)}, s32[1024]{0:T(1024)}, u32[]{:S(2)}) copy-start(s32[1024]{0:T(1024)} %param.9) | copy-start | bytes 12292
  7.2 8.8 %copy-start.1 = (s32[1024]{0:T(1024)S(1)}, s32[1024]{0:T(1024)}, u32[]{:S(2)}) copy-start(s32[1024]{0:T(1024)} %param.8) | copy-start | bytes 12292
  7.2 169.9 %all-to-all-start = ((bf16[8,448,2048]{2,1,0:T(8,128)(2,1)}), bf16[8,448,2048]{2,1,0:T(8,128)(2,1)}, u32[]{:S(2)}, u32[]{:S(2)}) async-start(bf16[8,448,2048]{2,1,0:T(8,128)(2,1)} %stack.2), calls=%async_computation | async-start | bytes 29360128 | tf_op jit(solution)/shard_map/all_to_all | solution.py:16
  177.1 7.6 %copy-start.2 = (bf16[3584,512]{1,0:T(8,128)(2,1)S(1)}, bf16[3584,512]{1,0:T(8,128)(2,1)}, u32[]{:S(2)}) copy-start(bf16[3584,512]{1,0:T(8,128)(2,1)} %param.10) | copy-start | bytes 11010052
